TPU v7x, 512 devices: a whole 4x4x16 slice. The times are simulated.
512 devices in a mesh: aux: 16 (over z_lo, y), row: 32 (over x, z_hi, core).
Axes of the slice: x: 4, y: 4, z: 16 (z_hi: 4, z_lo: 4; z = z_hi * 4 + z_lo), core: 2. Of those that a mesh axis runs over, the one named last changes fastest.
Arguments:
- coeff: bfloat16 [800, 4096], P(None, 'row'), may hold values from -0.109375 to 0.109375
- band: bfloat16 [32, 384, 4096], P('aux', None, 'row'), may hold values from -6 to 6
- pairs: int32 [32, 32], replicated, may hold values from 0 to 1, as said below
Outputs:
- exchange_k: float32 [4096, 4096], P('row', 'aux')
Inputs may be any that keep to these rules, and one draw needn't show every extreme that they name: pairs is symmetric, holds only 0 and 1, and its diagonal is 1; how many blocks a row keeps differs from row to row.
All inputs are finite; a program needn't handle non-finite values.
Results may differ from a plain program's by a relative error of at most 0.0012.
Values may be sent and summed in bfloat16 or wider, within the bound.
No kernel may reach another device: no remote copies, remote signals or barrier semaphores. Data moves between devices by JAX's collectives and lax.ppermute only.
A program may use at most 64 MiB of HBM per device.

v0:
```python
import jax
import jax.numpy as jnp
from jax import lax
from jax.sharding import Mesh
from jax.sharding import PartitionSpec as P

ROW = ("row_0", "row_1", "row_2")


def padded_2(cells, sides, width):
    for axis, dim in sides:
        count = lax.axis_size(axis)
        ends = count - 1
        head = lax.slice_in_dim(cells, 0, width, axis=dim)
        tail = lax.slice_in_dim(cells, cells.shape[dim] - width, cells.shape[dim], axis=dim)
        cells = jnp.concatenate(
            [
                lax.ppermute(tail, axis, [(i, (i + 1) % count) for i in range(ends)]),
                cells,
                lax.ppermute(head, axis, [((i + 1) % count, i) for i in range(ends)]),
            ],
            axis=dim,
        )
    return cells


def laid_out(blocks, dim):
    lengths = list(blocks.shape[1:])
    lengths[dim] *= blocks.shape[0]
    return jnp.moveaxis(blocks, 0, dim).reshape(lengths)


def gather_in_order(shard, axes, turns):
    blocks = shard[None]
    for k in turns:
        blocks = lax.all_gather(blocks, axes[k], axis=0, tiled=True)
    held = [lax.axis_size(axes[k]) for k in reversed(turns)]
    blocks = blocks.reshape(*held, *shard.shape)
    turned = sorted(range(len(turns)), key=lambda place: turns[len(turns) - 1 - place])
    return blocks.transpose(*turned, *range(len(turns), blocks.ndim)).reshape(-1, *shard.shape)


def whole_of(shard, axes, turns, dim):
    return laid_out(gather_in_order(shard, axes, turns), dim)


def in_blocks(shard, dim, devices):
    before, after = (shard.shape[:dim], shard.shape[dim + 1 :])
    return jnp.moveaxis(shard.reshape(*before, devices, -1, *after), dim, 0)


def sum_at_owner(shard, axis, dim):
    blocks = in_blocks(shard, dim, lax.axis_size(axis))
    arrived = lax.all_to_all(blocks, axis, split_axis=0, concat_axis=0, tiled=True)
    return arrived.sum(axis=0)


def on_device(coeff, band, pairs):
    block = band.shape[2]
    row_count = lax.axis_size(ROW)
    own_index = lax.axis_index(ROW)
    padded = padded_2(coeff, ((ROW, 1),), block)
    half_factor = jnp.einsum(
        "ij,qjm->qim", padded, band, preferred_element_type=jnp.float32
    ).astype(jnp.bfloat16)
    stacked = half_factor.reshape(-1, block)
    own_row = lax.dynamic_index_in_dim(pairs, own_index, 0, keepdims=False)
    piece = whole_of(stacked, ROW, (1, 0, 2), 1)
    product = lax.dot_general(
        stacked, piece, (((0,), (0,)), ((), ())), preferred_element_type=jnp.float32
    )
    column_block = jnp.arange(piece.shape[1], dtype=jnp.int32) // block
    onehot = (column_block[:, None] == jnp.arange(row_count, dtype=jnp.int32)[None, :]).astype(
        jnp.float32
    )
    screen = jnp.dot(onehot, own_row.astype(jnp.float32))
    k_rows = product * screen[None, :]
    return sum_at_owner(k_rows, "aux", 1)


def solution(mesh):
    torus = Mesh(
        mesh.devices.reshape(mesh.shape["aux"], 4, 4, 2), ("aux", "row_0", "row_1", "row_2")
    )
    in_specs = (P(None, ROW), P("aux", None, ROW), P())
    out_specs = P(ROW, "aux")
    return jax.shard_map(
        on_device, mesh=torus, in_specs=in_specs, out_specs=out_specs, check_vma=False
    )
```

profile of v0, /device:TPU:2, one launch (start us, length us, event | category | flops | bytes accessed | tf_op | source)
XLA Modules:
  0.0 297.3 jit_solution(3850492844797709839)
XLA Ops:
  6.5 0.0 copy-start
  6.5 0.0 all-gather.4.cloned.1.call-start
  6.5 12.3 %collective-permute-start.1 = (bf16[800,128]{1,0:T(8,128)(2,1)}, bf16[800,128]{1,0:T(8,128)(2,1)S(1)}, u32[]{:S(2)}, u32[]{:S(2)}) collective-permute-start(bf16[800,128]{1,0:T(8,128)(2,1)} %param.3), channel_id=1, source_target_pairs={{1,0},{2,1},{3,2},{4,3},{5,4},{6,5},{7,6},{8,7},{9,8},{10,9},{11,1... | collective-permute-start | bytes 614408 | tf_op jit(solution)/shard_map/ppermute | solution.py:20
  18.8 1.9 collective-permute-start
  20.7 8.3 %collective-permute-done.1 = bf16[800,128]{1,0:T(8,128)(2,1)S(1)} collective-permute-done((bf16[800,128]{1,0:T(8,128)(2,1)}, bf16[800,128]{1,0:T(8,128)(2,1)S(1)}, u32[]{:S(2)}, u32[]{:S(2)}) %collective-permute-start.1) | collective-permute-done | bytes 204832 | tf_op jit(solution)/shard_map/ppermute | solution.py:20
  29.0 8.6 %collective-permute-done = bf16[800,128]{1,0:T(8,128)(2,1)S(1)} collective-permute-done((bf16[800,128]{1,0:T(8,128)(2,1)}, bf16[800,128]{1,0:T(8,128)(2,1)S(1)}, u32[]{:S(2)}, u32[]{:S(2)}) %collective-permute-start) | collective-permute-done | bytes 204832 | tf_op jit(solution)/shard_map/ppermute | solution.py:18
  37.6 0.0 copy-done
  37.6 2.1 convolution_convert_fusion
  39.7 0.0 all-gather.4.cloned.1.call-update
  39.7 0.0 all-gather.6.cloned.1.call-start
  39.8 72.0 %all-gather.4.cloned.1.call-done = bf16[4,1600,128]{2,1,0:T(8,128)(2,1)} async-done(((bf16[1,1600,128]{2,1,0:T(8,128)(2,1)}), bf16[4,1600,128]{2,1,0:T(8,128)(2,1)}) %all-gather.4.cloned.1.call-update) | async-done | bytes 1638416 | tf_op jit(solution)/shard_map/all_gather | solution.py:36
  111.8 0.0 all-gather.6.cloned.1.call-update
  111.8 0.0 all-gather.8.cloned.1.call-start
  111.9 73.6 %all-gather.6.cloned.1.call-done = bf16[16,1600,128]{2,1,0:T(8,128)(2,1)} async-done(((bf16[4,1600,128]{2,1,0:T(8,128)(2,1)}), bf16[16,1600,128]{2,1,0:T(8,128)(2,1)}) %all-gather.6.cloned.1.call-update) | async-done | bytes 6553616 | tf_op jit(solution)/shard_map/all_gather | solution.py:36
  185.5 0.0 all-gather.8.cloned.1.call-update
  185.5 0.9 fusion.10
  186.4 38.0 %all-gather.8.cloned.1.call-done = bf16[32,1600,128]{2,1,0:T(8,128)(2,1)} async-done(((bf16[16,1600,128]{2,1,0:T(8,128)(2,1)}), bf16[32,1600,128]{2,1,0:T(8,128)(2,1)}) %all-gather.8.cloned.1.call-update) | async-done | bytes 13107216 | tf_op jit(solution)/shard_map/all_gather | solution.py:36
  224.4 0.0 copy-start.1
  224.4 6.6 %copy.10 = bf16[4,4,2,1600,128]{4,3,2,1,0:T(8,128)(2,1)S(1)} copy(bf16[4,4,2,1600,128]{4,3,1,0,2:T(8,128)(2,1)} %bitcast.34) | data formatting | bytes 26214400 | tf_op jit(solution)/shard_map/transpose | solution.py:40
  231.0 0.0 copy-done.1
  231.0 2.1 fusion.3
  233.1 0.2 copy.22
  233.3 56.7 %all_to_all.5 = f32[16,128,256]{2,1,0:T(8,128)S(1)} all-to-all(f32[16,128,256]{2,1,0:T(8,128)S(1)} %bitcast.36), channel_id=1, replica_groups=mesh['aux'=16,'row_0'=4,'row_1'=4,'row_2'=2] {'aux'}, dimensions={0} | all-to-all | bytes 4194304 | tf_op jit(solution)/shard_map/all_to_all | solution.py:54
  290.0 0.8 reduce_sum.9
  (1 shorter events, 0.0 us)
Async XLA Ops:
  6.5 31.1 %copy-start = (bf16[2,384,128]{2,1,0:T(8,128)(2,1)S(1)}, bf16[2,384,128]{2,1,0:T(8,128)(2,1)}, u32[]{:S(2)}) copy-start(bf16[2,384,128]{2,1,0:T(8,128)(2,1)} %param.4) | copy-start | bytes 589828
  6.5 105.2 %all-gather.4.cloned.1.call-start = ((), (), s32[]{:S(2)}) async-start(), calls=%async_computation.1 | async-start | bytes 2048000 | tf_op jit(solution)/shard_map/all_gather | solution.py:36
  6.5 22.5 %collective-permute-start.1 = (bf16[800,128]{1,0:T(8,128)(2,1)}, bf16[800,128]{1,0:T(8,128)(2,1)S(1)}, u32[]{:S(2)}, u32[]{:S(2)}) collective-permute-start(bf16[800,128]{1,0:T(8,128)(2,1)} %param.3), channel_id=1, source_target_pairs={{1,0},{2,1},{3,2},{4,3},{5,4},{6,5},{7,6},{8,7},{9,8},{10,9},{11,1... | collective-permute-start | bytes 614408 | tf_op jit(solution)/shard_map/ppermute | solution.py:20
  18.8 18.8 %collective-permute-start = (bf16[800,128]{1,0:T(8,128)(2,1)}, bf16[800,128]{1,0:T(8,128)(2,1)S(1)}, u32[]{:S(2)}, u32[]{:S(2)}) collective-permute-start(bf16[800,128]{1,0:T(8,128)(2,1)} %param.3), channel_id=1, source_target_pairs={{0,1},{1,2},{2,3},{3,4},{4,5},{5,6},{6,7},{7,8},{8,9},{9,10},{10,1... | collective-permute-start | bytes 614408 | tf_op jit(solution)/shard_map/ppermute | solution.py:18
  39.7 145.8 %all-gather.6.cloned.1.call-start = ((), (), s32[]{:S(2)}) async-start(), calls=%async_computation.2 | async-start | bytes 8192000 | tf_op jit(solution)/shard_map/all_gather | solution.py:36
  111.8 112.6 %all-gather.8.cloned.1.call-start = ((), (), s32[]{:S(2)}) async-start(), calls=%async_computation.3 | async-start | bytes 19660800 | tf_op jit(solution)/shard_map/all_gather | solution.py:36
  224.4 6.6 %copy-start.1 = (bf16[800,2,128]{2,0,1:T(8,128)(2,1)S(1)}, bf16[800,2,128]{2,0,1:T(8,128)(2,1)}, u32[]{:S(2)}) copy-start(bf16[800,2,128]{2,0,1:T(8,128)(2,1)} %convolution_convert_fusion) | copy-start | bytes 1228804
Sparse Core Ops, SparseCore 0:
  39.8 71.9 all-gather.3
  113.9 71.5 all-gather.5
  187.6 36.7 all-gather.7
where the time goes:
time: 298 us; the launch traced here: 297 us
  waiting for transfers between devices  201 us (67%)
  blocking collectives  56.7 us (19%)
  starting transfers between devices  14.3 us (5%)
  between operations  13.2 us (4%)
  local copies, waits for them, and re-layouts  6.8 us (2%)
  matrix products  5.05 us (2%)
    all_gather x3, waiting for transfers between devices, gather_in_order(): blocks = lax.all_gather(blocks, axes[k], axis=0, tiled=True)  184 us
    all_to_all x1, blocking collectives, sum_at_owner(): lax.all_to_all(blocks, axis, split_axis=0, concat_axis=0, tiled=True)  56.7 us
    ppermute x1, starting transfers between devices, padded_2(): lax.ppermute(head, axis, [((i + 1) % count, i) for i in range(ends)])  12.3 us
    ppermute x1, waiting for transfers between devices, padded_2(): lax.ppermute(tail, axis, [(i, (i + 1) % count) for i in range(ends)])  8.6 us
    ppermute x1, waiting for transfers between devices, padded_2(): lax.ppermute(head, axis, [((i + 1) % count, i) for i in range(ends)])  8.28 us
    transpose x1, local copies, waits for them, and re-layouts, gather_in_order(): blocks.transpose(*turned, *range(len(turns), blocks.ndim))  6.59 us
  transfers between devices with their start and end apart: 5, of which 5 were waited for; matrix products, arithmetic and copies ran while one was open for 0% of the time, Pallas kernels for 0%

commit v1 on v0

--- a/solution.py
+++ b/solution.py
@@ -33,7 +33,9 @@
 def gather_in_order(shard, axes, turns):
     blocks = shard[None]
     for k in turns:
-        blocks = lax.all_gather(blocks, axes[k], axis=0, tiled=True)
+        blocks = jnp.concatenate(
+            lax.all_to_all(jnp.stack([blocks] * lax.axis_size(axes[k])), axes[k], 0, 0), axis=0
+        )
     held = [lax.axis_size(axes[k]) for k in reversed(turns)]
     blocks = blocks.reshape(*held, *shard.shape)
     turned = sorted(range(len(turns)), key=lambda place: turns[len(turns) - 1 - place])

time: 298 us -> 274 us (0.919)
  the two profiles are of different devices: /device:TPU:2 before, /device:TPU:32 now
where the time goes in v1:
time: 274 us; the launch traced here: 273 us
  blocking collectives  173 us (63%)
  waiting for transfers between devices  67.8 us (25%)
  starting transfers between devices  14.8 us (5%)
  other arithmetic  7.26 us (3%)
  local copies, waits for them, and re-layouts  6.1 us (2%)
  matrix products  4.29 us (2%)
    all_to_all x2, blocking collectives, gather_in_order(): lax.all_to_all(jnp.stack([blocks] * lax.axis_size(axes[k])), axes[k], 0, 0)  113 us
    all_to_all x1, waiting for transfers between devices, gather_in_order(): lax.all_to_all(jnp.stack([blocks] * lax.axis_size(axes[k])), axes[k], 0, 0)  66.5 us
    all_to_all x1, blocking collectives, sum_at_owner(): lax.all_to_all(blocks, axis, split_axis=0, concat_axis=0, tiled=True)  60.1 us
    all_to_all x1, starting transfers between devices, gather_in_order(): lax.all_to_all(jnp.stack([blocks] * lax.axis_size(axes[k])), axes[k], 0, 0)  10.4 us
    another operation x1, other arithmetic, gather_in_order(): jnp.stack([blocks] * lax.axis_size(axes[k]))  6.47 us
  transfers between devices with their start and end apart: 3, of which 2 were waited for; matrix products, arithmetic and copies ran while one was open for 0% of the time, Pallas kernels for 0%

profile of v1, /device:TPU:32, one launch (start us, length us, event | category | flops | bytes accessed | tf_op | source)
XLA Modules:
  0.0 273.4 jit_solution(1958488849572521753)
XLA Ops:
  0.0 0.0 copy-start
  0.0 1.4 collective-permute-start.1
  1.4 3.0 %collective-permute-start = (bf16[800,128]{1,0:T(8,128)(2,1)}, bf16[800,128]{1,0:T(8,128)(2,1)S(1)}, u32[]{:S(2)}, u32[]{:S(2)}) collective-permute-start(bf16[800,128]{1,0:T(8,128)(2,1)} %param.3), channel_id=1, source_target_pairs={{0,1},{1,2},{2,3},{3,4},{4,5},{5,6},{6,7},{7,8},{8,9},{9,10},{10,1... | collective-permute-start | bytes 614408 | tf_op jit(solution)/shard_map/ppermute | solution.py:18
  4.5 0.0 collective-permute-done.1
  4.5 1.3 collective-permute-done
  5.7 0.0 copy-done
  5.7 1.3 convolution_convert_fusion
  7.0 0.2 stack.9
  7.3 90.7 %all_to_all.20 = bf16[4,1,1600,128]{3,2,1,0:T(8,128)(2,1)S(1)} all-to-all(bf16[4,1,1600,128]{3,2,1,0:T(8,128)(2,1)S(1)} %stack.9), channel_id=1, replica_groups=mesh['aux'=16,'row_0'=4,'row_1'=4,'row_2'=2] {'row_1'}, dimensions={0} | all-to-all | bytes 3276800 | tf_op jit(solution)/shard_map/all_to_all | solution.py:37
  98.0 4.0 %stack.10 = bf16[4,4,1600,128]{3,2,1,0:T(8,128)(2,1)} broadcast(bf16[4,1600,128]{2,1,0:T(8,128)(2,1)S(1)} %bitcast.37), dimensions={1,2,3} | broadcast | bytes 8192000 | tf_op jit(solution)/shard_map/stack | solution.py:37
  101.9 10.4 %all-to-all-start.1 = ((bf16[4,4,1600,128]{3,2,1,0:T(8,128)(2,1)}), bf16[4,4,1600,128]{3,2,1,0:T(8,128)(2,1)}, u32[]{:S(2)}, u32[]{:S(2)}) async-start(bf16[4,4,1600,128]{3,2,1,0:T(8,128)(2,1)} %stack.10), calls=%async_computation.1 | async-start | bytes 13107200 | tf_op jit(solution)/shard_map/all_to_all | solution.py:37
  112.3 0.9 fusion.10
  113.2 66.5 %all-to-all-done.1 = bf16[4,4,1600,128]{3,2,1,0:T(8,128)(2,1)} async-done(((bf16[4,4,1600,128]{3,2,1,0:T(8,128)(2,1)}), bf16[4,4,1600,128]{3,2,1,0:T(8,128)(2,1)}, u32[]{:S(2)}, u32[]{:S(2)}) %all-to-all-start.1) | async-done | bytes 6553632 | tf_op jit(solution)/shard_map/all_to_all | solution.py:37
  179.8 6.5 %pad_maximum_fusion = bf16[2,16,1600,128]{3,2,1,0:T(8,128)(2,1)S(1)} fusion(bf16[1,16,1600,128]{3,2,1,0:T(8,128)(2,1)} %bitcast.5), kind=kLoop, calls=%fused_computation.3 | loop fusion | flops 6553600 | bytes 19660800 | tf_op jit(solution)/shard_map/stack | solution.py:37
  186.2 22.3 %all_to_all.21 = bf16[2,16,1600,128]{3,2,1,0:T(8,128)(2,1)S(1)} all-to-all(bf16[2,16,1600,128]{3,2,1,0:T(8,128)(2,1)S(1)} %pad_maximum_fusion), channel_id=1, replica_groups=mesh['aux'=16,'row_0'=4,'row_1'=4,'row_2'=2] {'row_2'}, dimensions={0} | all-to-all | bytes 26214400 | tf_op jit(solution)/shard_map/all_to_all | solution.py:37
  208.5 1.7 copy.8
  210.2 2.1 fusion.3
  212.4 0.2 copy.20
  212.6 60.1 %all_to_all.22 = f32[16,128,256]{2,1,0:T(8,128)S(1)} all-to-all(f32[16,128,256]{2,1,0:T(8,128)S(1)} %bitcast.36), channel_id=1, replica_groups=mesh['aux'=16,'row_0'=4,'row_1'=4,'row_2'=2] {'aux'}, dimensions={0} | all-to-all | bytes 4194304 | tf_op jit(solution)/shard_map/all_to_all | solution.py:56
  272.7 0.8 reduce_sum.9
  (1 shorter events, 0.0 us)
Async XLA Ops:
  0.0 5.7 %copy-start = (bf16[2,384,128]{2,1,0:T(8,128)(2,1)S(1)}, bf16[2,384,128]{2,1,0:T(8,128)(2,1)}, u32[]{:S(2)}) copy-start(bf16[2,384,128]{2,1,0:T(8,128)(2,1)} %param.4) | copy-start | bytes 589828
  0.0 4.5 %collective-permute-start.1 = (bf16[800,128]{1,0:T(8,128)(2,1)}, bf16[800,128]{1,0:T(8,128)(2,1)S(1)}, u32[]{:S(2)}, u32[]{:S(2)}) collective-permute-start(bf16[800,128]{1,0:T(8,128)(2,1)} %param.3), channel_id=1, source_target_pairs={{1,0},{2,1},{3,2},{4,3},{5,4},{6,5},{7,6},{8,7},{9,8},{10,9},{11,1... | collective-permute-start | bytes 614408 | tf_op jit(solution)/shard_map/ppermute | solution.py:20
  1.4 4.3 %collective-permute-start = (bf16[800,128]{1,0:T(8,128)(2,1)}, bf16[800,128]{1,0:T(8,128)(2,1)S(1)}, u32[]{:S(2)}, u32[]{:S(2)}) collective-permute-start(bf16[800,128]{1,0:T(8,128)(2,1)} %param.3), channel_id=1, source_target_pairs={{0,1},{1,2},{2,3},{3,4},{4,5},{5,6},{6,7},{7,8},{8,9},{9,10},{10,1... | collective-permute-start | bytes 614408 | tf_op jit(solution)/shard_map/ppermute | solution.py:18
  101.9 77.8 %all-to-all-start.1 = ((bf16[4,4,1600,128]{3,2,1,0:T(8,128)(2,1)}), bf16[4,4,1600,128]{3,2,1,0:T(8,128)(2,1)}, u32[]{:S(2)}, u32[]{:S(2)}) async-start(bf16[4,4,1600,128]{3,2,1,0:T(8,128)(2,1)} %stack.10), calls=%async_computation.1 | async-start | bytes 13107200 | tf_op jit(solution)/shard_map/all_to_all | solution.py:37
